TPU v7x, 32 devices: a whole 2x2x4 slice. The times are simulated.
32 devices in a mesh: tile: 8 (over y, x, core), head: 4 (over z).
Axes of the slice: x: 2, y: 2, z: 4, core: 2. Of those that a mesh axis runs over, the one named last changes fastest.
Arguments:
- latent: bfloat16 [16, 512, 512], P('tile', 'head'), may hold values from -6 to 6
- norm1_gain: float32 [512], replicated, may hold values from 0.25 to 1.75
- norm1_shift: float32 [512], replicated, may hold values from -1.75 to 1.75
- conv1_weight: bfloat16 [3, 3, 512, 512], replicated, may hold values from -0.09375 to 0.09375
- conv1_bias: float32 [512], replicated, may hold values from -1.75 to 1.75
- norm2_gain: float32 [512], replicated, may hold values from 0.25 to 1.75
- norm2_shift: float32 [512], replicated, may hold values from -1.75 to 1.75
- conv2_weight: bfloat16 [3, 3, 512, 512], replicated, may hold values from -0.09375 to 0.09375
- conv2_bias: float32 [512], replicated, may hold values from -1.75 to 1.75
- norm3_gain: float32 [512], replicated, may hold values from 0.25 to 1.75
- norm3_shift: float32 [512], replicated, may hold values from -1.75 to 1.75
- query_weight: bfloat16 [512, 512], replicated, may hold values from -2 to 2
- query_bias: float32 [512], replicated, may hold values from -3 to 3
- key_weight: bfloat16 [512, 512], replicated, may hold values from -2 to 2
- value_weight: bfloat16 [512, 512], replicated, may hold values from -0.25 to 0.25
- value_bias: float32 [512], replicated, may hold values from -3 to 3
- out_weight: bfloat16 [512, 512], replicated, may hold values from -0.5 to 0.5
- out_bias: float32 [512], replicated, may hold values from -1.75 to 1.75
Outputs:
- block_out: bfloat16 [16, 512, 512], P('tile', 'head')
All inputs are finite; a program needn't handle non-finite values.
Results may differ from a plain program's by a relative error of at most 0.01615.
Values may be sent and summed in bfloat16 or wider, within the bound.
A program may use at most 128 MiB of HBM per device.

v0:
```python
import jax
import jax.numpy as jnp
from jax import lax
from jax.sharding import PartitionSpec as P

C = 512
GROUPS = 32


def extended(x, sides, width):
    for axis, dim in sides:
        peers, length = (lax.axis_size(axis), x.shape[dim])
        up = [(i, (i + 1) % peers) for i in range(peers - 1)]
        down = [(j, i) for i, j in up]
        last = lax.slice_in_dim(x, length - width, length, axis=dim)
        initial = lax.slice_in_dim(x, 0, width, axis=dim)
        before = lax.ppermute(last, axis, up)
        after = lax.ppermute(initial, axis, down)
        x = jnp.concatenate([before, x, after], axis=dim)
    return x


def group_norm(values, gain, shift, members):
    grouped = values.reshape(-1, GROUPS, C // GROUPS)
    sums = lax.psum(jnp.sum(grouped, axis=(0, 2)), ("tile", "head"))
    mean = sums / members
    deviation = grouped - mean[None, :, None]
    variance = lax.psum(jnp.sum(deviation * deviation, axis=(0, 2)), ("tile", "head")) / members
    normalized = deviation * lax.rsqrt(variance + 1e-06)[None, :, None]
    return normalized.reshape(values.shape) * gain + shift


def conv_three(act, weight, bias):
    padded = extended(act, (("tile", 0), ("head", 1)), 1)
    result = lax.conv_general_dilated(
        padded[None],
        weight,
        (1, 1),
        "VALID",
        dimension_numbers=("NHWC", "HWIO", "NHWC"),
        preferred_element_type=jnp.float32,
    )[0]
    return result + bias


def per_device(
    latent,
    norm1_gain,
    norm1_shift,
    conv1_weight,
    conv1_bias,
    norm2_gain,
    norm2_shift,
    conv2_weight,
    conv2_bias,
    norm3_gain,
    norm3_shift,
    query_weight,
    query_bias,
    key_weight,
    value_weight,
    value_bias,
    out_weight,
    out_bias,
):
    local_rows, local_cols, channels = latent.shape
    positions = local_rows * local_cols
    members = positions * lax.axis_size("tile") * lax.axis_size("head") * (C // GROUPS)
    latent32 = latent.astype(jnp.float32).reshape(positions, C)
    act1 = jax.nn.silu(group_norm(latent32, norm1_gain, norm1_shift, members)).astype(jnp.bfloat16)
    hidden = conv_three(act1.reshape(local_rows, local_cols, C), conv1_weight, conv1_bias).reshape(
        positions, C
    )
    act2 = jax.nn.silu(group_norm(hidden, norm2_gain, norm2_shift, members)).astype(jnp.bfloat16)
    second = conv_three(act2.reshape(local_rows, local_cols, C), conv2_weight, conv2_bias).reshape(
        positions, C
    )
    resid = (latent32 + second).astype(jnp.bfloat16)
    normed = group_norm(resid.astype(jnp.float32), norm3_gain, norm3_shift, members).astype(
        jnp.bfloat16
    )
    queries = (
        jnp.dot(normed, query_weight, preferred_element_type=jnp.float32) + query_bias
    ).astype(jnp.bfloat16)
    tile_queries = lax.all_gather(queries, "head", axis=0, tiled=True)
    query_rows = tile_queries.shape[0]
    softmax_scale = 1.0 / C**0.5
    widest = positions * max(1, 2048 // positions)
    initial = (
        jnp.full((query_rows,), -1e30, jnp.float32),
        jnp.zeros((query_rows,), jnp.float32),
        jnp.zeros((query_rows, C), jnp.float32),
    )
    keys = jnp.dot(normed, key_weight, preferred_element_type=jnp.float32).astype(jnp.bfloat16)
    values = (
        jnp.dot(normed, value_weight, preferred_element_type=jnp.float32) + value_bias
    ).astype(jnp.bfloat16)
    key_rows = lax.all_gather(keys, "tile", axis=0, tiled=True)
    rows_here = key_rows.shape[0]
    block_len = min(rows_here, widest)
    while rows_here % block_len != 0:
        block_len = block_len - positions
    nblocks = rows_here // block_len

    def step_block(state_in, block_pair):
        run_max, run_sum, weighted = state_in
        key_block, value_block = block_pair
        scores = (
            jnp.dot(tile_queries, key_block.T, preferred_element_type=jnp.float32) * softmax_scale
        )
        new_max = jnp.maximum(run_max, jnp.max(scores, axis=1))
        factor = jnp.exp(run_max - new_max)
        expo = jnp.exp(scores - new_max[:, None])
        run_sum = run_sum * factor + jnp.sum(expo, axis=1)
        weighted = weighted * factor[:, None] + jnp.dot(
            expo.astype(jnp.bfloat16), value_block, preferred_element_type=jnp.float32
        )
        return ((new_max, run_sum, weighted), None)

    blocked = (
        key_rows.reshape(nblocks, block_len, C),
        lax.all_gather(values, "tile", axis=0, tiled=True).reshape(nblocks, block_len, C),
    )
    state_out, unused = lax.scan(step_block, initial, blocked)
    run_max, run_sum, weighted = state_out
    top = lax.pmax(run_max, "head")
    factor = jnp.exp(run_max - top)
    own_weighted, own_sum = (
        lax.psum_scatter(
            (weighted * factor[:, None]).astype(jnp.bfloat16),
            "head",
            scatter_dimension=0,
            tiled=True,
        ).astype(jnp.float32),
        lax.psum_scatter(
            (run_sum * factor).astype(jnp.bfloat16), "head", scatter_dimension=0, tiled=True
        ).astype(jnp.float32),
    )
    attended = (own_weighted / own_sum[:, None]).astype(jnp.bfloat16)
    mixed = (
        resid.astype(jnp.float32)
        + jnp.dot(attended, out_weight, preferred_element_type=jnp.float32)
        + out_bias
    )
    return mixed.astype(jnp.bfloat16).reshape(local_rows, local_cols, C)


def solution(mesh):
    return jax.shard_map(
        per_device,
        mesh=mesh,
        in_specs=(
            P("tile", "head", None),
            P(),
            P(),
            P(),
            P(),
            P(),
            P(),
            P(),
            P(),
            P(),
            P(),
            P(),
            P(),
            P(),
            P(),
            P(),
            P(),
            P(),
        ),
        out_specs=P("tile", "head", None),
        check_vma=False,
    )
```

profile of v0, /device:TPU:0, one launch (start us, length us, event | category | flops | bytes accessed | tf_op | source)
XLA Modules:
  0.0 429.3 jit_solution(8962881131567020059)
XLA Ops:
  7.8 42.0 %psum.42 = f32[32]{0:T(128)S(1)} all-reduce(f32[32]{0:T(128)S(1)} %reduce_sum.83), channel_id=1, replica_groups=mesh['tile'=8,'head'=4] {'tile','head'}, use_global_device_ids=true, to_apply=%region_2.0 | all-reduce | flops 32 | bytes 256 | tf_op jit(solution)/shard_map/psum | solution.py:25
  51.2 40.1 %psum.43 = f32[32]{0:T(128)S(1)} all-reduce(f32[32]{0:T(128)S(1)} %reduce_sum.89), channel_id=1, replica_groups=mesh['tile'=8,'head'=4] {'tile','head'}, use_global_device_ids=true, to_apply=%region_5.6 | all-reduce | flops 32 | bytes 256 | tf_op jit(solution)/shard_map/psum | solution.py:28
  91.5 1.2 fusion.63
  92.7 1.3 collective-permute-start
  94.0 1.3 collective-permute-start.1
  95.3 1.2 fusion.54
  96.5 3.3 collective-permute-done.1
  99.8 2.6 collective-permute-start.2
  102.4 1.3 collective-permute-start.3
  103.8 4.2 collective-permute-done.3
  108.8 1.5 select_reduce_fusion.1
  110.5 42.0 %psum.44 = f32[32]{0:T(128)S(1)} all-reduce(f32[32]{0:T(128)S(1)} %reduce_sum.92), channel_id=1, replica_groups=mesh['tile'=8,'head'=4] {'tile','head'}, use_global_device_ids=true, to_apply=%region_8.9 | all-reduce | flops 32 | bytes 256 | tf_op jit(solution)/shard_map/psum | solution.py:25
  153.5 39.9 %psum.45 = f32[32]{0:T(128)S(1)} all-reduce(f32[32]{0:T(128)S(1)} %reduce_sum.117), channel_id=1, replica_groups=mesh['tile'=8,'head'=4] {'tile','head'}, use_global_device_ids=true, to_apply=%region_11.12 | all-reduce | flops 32 | bytes 256 | tf_op jit(solution)/shard_map/psum | solution.py:28
  194.0 1.3 collective-permute-start.4
  195.3 1.3 collective-permute-start.5
  196.8 4.2 collective-permute-done.5
  201.0 3.4 collective-permute-start.6
  204.4 1.3 collective-permute-start.7
  205.8 4.2 collective-permute-done.7
  210.8 3.8 convolution_select_fusion
  215.9 41.5 %psum.46 = f32[32]{0:T(128)S(1)} all-reduce(f32[32]{0:T(128)S(1)} %reduce_sum.120), channel_id=1, replica_groups=mesh['tile'=8,'head'=4] {'tile','head'}, use_global_device_ids=true, to_apply=%region_14.15 | all-reduce | flops 32 | bytes 256 | tf_op jit(solution)/shard_map/psum | solution.py:25
  258.0 40.5 %psum.47 = f32[32]{0:T(128)S(1)} all-reduce(f32[32]{0:T(128)S(1)} %reduce_sum.123), channel_id=1, replica_groups=mesh['tile'=8,'head'=4] {'tile','head'}, use_global_device_ids=true, to_apply=%region_17.18 | all-reduce | flops 32 | bytes 256 | tf_op jit(solution)/shard_map/psum | solution.py:28
  302.1 24.9 %all-gather.4.cloned.1.call-done = bf16[1024,512]{1,0:T(8,128)(2,1)} async-done(((bf16[256,512]{1,0:T(8,128)(2,1)}), bf16[1024,512]{1,0:T(8,128)(2,1)}) %all-gather.4.cloned.1.call-update) | async-done | bytes 1048592 | tf_op jit(solution)/shard_map/all_gather | solution.py:85
  327.0 29.1 %all-gather.6.cloned.1.call-done = bf16[2048,512]{1,0:T(8,128)(2,1)} async-done(((bf16[256,512]{1,0:T(8,128)(2,1)}), bf16[2048,512]{1,0:T(8,128)(2,1)}) %all-gather.6.cloned.1.call-update) | async-done | bytes 2097168 | tf_op jit(solution)/shard_map/all_gather | solution.py:98
  356.1 7.5 %multiply_reduce_fusion = (f32[1024]{0:T(1024)S(1)}, f32[1024,2048]{1,0:T(8,128)}) fusion(bf16[1024,512]{1,0:T(8,128)(2,1)} %all-gather.4.cloned.1.call-done, bf16[2048,512]{1,0:T(8,128)(2,1)} %all-gather.6.cloned.1.call-done), kind=kOutput, calls=%fused_computation.1 | convolution fusion | flops 2151676928 | bytes 11538432 | tf_op jit(solution)/shard_map/while/body/eval_jaxpr/dot_general | solution.py:109
  363.6 11.7 %pmax.7 = f32[1024]{0:T(1024)S(1)} all-reduce(f32[1024]{0:T(1024)S(1)} %broadcast_maximum_fusion), channel_id=1, replica_groups=mesh['tile'=8,'head'=4] {'head'}, use_global_device_ids=true, to_apply=%region_19.20 | all-reduce | flops 1024 | bytes 8192 | tf_op jit(solution)/shard_map/pmax | solution.py:126
  375.2 4.7 %fusion = f32[1024]{0:T(1024)S(1)} fusion(f32[1024,2048]{1,0:T(8,128)} %get-tuple-element.42, f32[1024]{0:T(1024)S(1)} %broadcast_maximum_fusion), kind=kLoop, calls=%fused_computation.2 | loop fusion | flops 6290432 | bytes 8396800 | tf_op jit(solution)/shard_map/while/body/eval_jaxpr/reduce_sum | solution.py:114
  380.0 5.8 %all-gather.8.cloned.1.call-done = bf16[2048,512]{1,0:T(8,128)(2,1)} async-done(((bf16[256,512]{1,0:T(8,128)(2,1)}), bf16[2048,512]{1,0:T(8,128)(2,1)}) %all-gather.8.cloned.1.call-update) | async-done | bytes 2097168 | tf_op jit(solution)/shard_map/all_gather | solution.py:122
  385.8 7.4 %multiply_convert_fusion = bf16[1024,512]{1,0:T(8,128)(2,1)} fusion(bf16[2048,512]{1,0:T(8,128)(2,1)} %all-gather.8.cloned.1.call-done, f32[1024,2048]{1,0:T(8,128)} %get-tuple-element.42, f32[1024]{0:T(1024)S(1)} %broadcast_maximum_fusion, f32[1024]{0:T(1024)S(1)} %get-tuple-element.18, f32[1024]{0:T(1024)S(1)} %get-tuple-element.38), kind=kOutput, calls=%fused_computation.7 | convolution fusion | flops 2155347968 | bytes 11546624 | tf_op jit(solution)/shard_map/while/body/eval_jaxpr/dot_general | solution.py:115
  394.5 12.1 %all-reduce = bf16[1024]{0:T(1024)(128)(2,1)S(1)} all-reduce(bf16[1024]{0:T(1024)(128)(2,1)S(1)} %get-tuple-element.17), channel_id=3, replica_groups=mesh['tile'=8,'head'=4] {'head'}, use_global_device_ids=true, to_apply=%region_22.23.clone | all-reduce | flops 1024 | bytes 4096
  406.6 14.1 %reduce-scatter.2.cloned.1.call-done = bf16[256,512]{1,0:T(8,128)(2,1)} async-done(((bf16[1024,512]{1,0:T(8,128)(2,1)}), bf16[256,512]{1,0:T(8,128)(2,1)}) %reduce-scatter.2.cloned.1.call-update) | async-done | bytes 262160 | tf_op jit(solution)/shard_map/reduce_scatter | solution.py:129
  420.7 2.0 fusion.11
  (111 shorter events, 12.3 us)
Async XLA Ops:
  6.5 292.2 %copy-start = (bf16[512,512]{1,0:T(8,128)(2,1)S(1)}, bf16[512,512]{1,0:T(8,128)(2,1)}, u32[]{:S(2)}) copy-start(bf16[512,512]{1,0:T(8,128)(2,1)} %param.29) | copy-start | bytes 1572868
  6.5 320.4 %all-gather.4.cloned.1.call-start = ((), (), s32[]{:S(2)}) async-start(), calls=%async_computation.1 | async-start | bytes 1310720 | tf_op jit(solution)/shard_map/all_gather | solution.py:85
  92.7 3.8 collective-permute-start
  94.0 5.7 %collective-permute-start.1 = (bf16[1,128,512]{2,1,0:T(8,128)(2,1)S(1)}, bf16[1,128,512]{2,1,0:T(8,128)(2,1)S(1)}, u32[]{:S(2)}, u32[]{:S(2)}) collective-permute-start(bf16[1,128,512]{2,1,0:T(8,128)(2,1)S(1)} %get-tuple-element.37), channel_id=1, source_target_pairs={{4,0},{8,4},{12,8},{16,12},{20,16},{24,20},{28,24},{5,1},{9,5},{13... | collective-permute-start | bytes 393224 | tf_op jit(solution)/shard_map/ppermute | solution.py:18
  99.7 9.0 %copy-start.7 = (bf16[3,3,512,512]{3,2,1,0:T(8,128)(2,1)S(1)}, bf16[3,3,512,512]{3,2,1,0:T(8,128)(2,1)}, u32[]{:S(2)}) copy-start(bf16[3,3,512,512]{3,2,1,0:T(8,128)(2,1)} %param.21) | copy-start | bytes 14155780
  99.8 4.0 collective-permute-start.2
  102.4 6.4 %copy-start.2 = (f32[512]{0:T(512)S(1)}, f32[512]{0:T(512)}, u32[]{:S(2)}) copy-start(f32[512]{0:T(512)} %param.22) | copy-start | bytes 6148
  102.4 6.4 %copy-start.6 = (pred[8,17]{0,1:T(8,128)(4,1)S(1)}, pred[8,17]{0,1:T(8,128)(4,1)}, u32[]{:S(2)}) copy-start(pred[8,17]{0,1:T(8,128)(4,1)} %constant.47) | copy-start | bytes 412
  102.4 5.5 %collective-permute-start.3 = (bf16[4,1,512]{2,1,0:T(2,128)(2,1)S(1)}, bf16[4,1,512]{2,1,0:T(2,128)(2,1)S(1)}, u32[]{:S(2)}, u32[]{:S(2)}) collective-permute-start(bf16[4,1,512]{2,1,0:T(2,128)(2,1)S(1)} %get-tuple-element.33), channel_id=1, source_target_pairs={{1,0},{2,1},{3,2},{5,4},{6,5},{7,6},{9,8},{10,9},{11,10},{13,12},{... | collective-permute-start | bytes 12296 | tf_op jit(solution)/shard_map/ppermute | solution.py:18
  110.3 83.4 %copy-start.3 = (f32[512]{0:T(512)S(1)}, f32[512]{0:T(512)}, u32[]{:S(2)}) copy-start(f32[512]{0:T(512)} %param.24) | copy-start | bytes 6148
  110.3 83.4 %copy-start.4 = (f32[512]{0:T(512)S(1)}, f32[512]{0:T(512)}, u32[]{:S(2)}) copy-start(f32[512]{0:T(512)} %param.23) | copy-start | bytes 6148
  194.0 2.8 collective-permute-start.4
  195.3 5.7 %collective-permute-start.5 = (bf16[1,128,512]{2,1,0:T(8,128)(2,1)S(1)}, bf16[1,128,512]{2,1,0:T(8,128)(2,1)S(1)}, u32[]{:S(2)}, u32[]{:S(2)}) collective-permute-start(bf16[1,128,512]{2,1,0:T(8,128)(2,1)S(1)} %get-tuple-element.35), channel_id=1, source_target_pairs={{4,0},{8,4},{12,8},{16,12},{20,16},{24,20},{28,24},{5,1},{9,5},{13... | collective-permute-start | bytes 393224 | tf_op jit(solution)/shard_map/ppermute | solution.py:18
  201.0 4.8 %collective-permute-start.6 = (bf16[4,1,512]{2,1,0:T(2,128)(2,1)S(1)}, bf16[4,1,512]{2,1,0:T(2,128)(2,1)S(1)}, u32[]{:S(2)}, u32[]{:S(2)}) collective-permute-start(bf16[4,1,512]{2,1,0:T(2,128)(2,1)S(1)} %get-tuple-element.28), channel_id=1, source_target_pairs={{0,1},{1,2},{2,3},{4,5},{5,6},{6,7},{8,9},{9,10},{10,11},{12,13},{... | collective-permute-start | bytes 12296 | tf_op jit(solution)/shard_map/ppermute | solution.py:17
  204.4 5.5 %collective-permute-start.7 = (bf16[4,1,512]{2,1,0:T(2,128)(2,1)S(1)}, bf16[4,1,512]{2,1,0:T(2,128)(2,1)S(1)}, u32[]{:S(2)}, u32[]{:S(2)}) collective-permute-start(bf16[4,1,512]{2,1,0:T(2,128)(2,1)S(1)} %get-tuple-element.30), channel_id=1, source_target_pairs={{1,0},{2,1},{3,2},{5,4},{6,5},{7,6},{9,8},{10,9},{11,10},{13,12},{... | collective-permute-start | bytes 12296 | tf_op jit(solution)/shard_map/ppermute | solution.py:18
  214.6 1.0 copy-start.1
  214.6 0.9 copy-start.5
  215.1 83.7 %copy-start.11 = (f32[512]{0:T(512)S(1)}, f32[512]{0:T(512)}, u32[]{:S(2)}) copy-start(f32[512]{0:T(512)} %param.30) | copy-start | bytes 6148
  215.1 83.7 %copy-start.12 = (f32[512]{0:T(512)S(1)}, f32[512]{0:T(512)}, u32[]{:S(2)}) copy-start(f32[512]{0:T(512)} %param.28) | copy-start | bytes 6148
  215.1 83.7 %copy-start.13 = (f32[512]{0:T(512)S(1)}, f32[512]{0:T(512)}, u32[]{:S(2)}) copy-start(f32[512]{0:T(512)} %param.27) | copy-start | bytes 6148
  257.6 42.3 %copy-start.8 = (bf16[512,512]{1,0:T(8,128)(2,1)S(1)}, bf16[512,512]{1,0:T(8,128)(2,1)}, u32[]{:S(2)}) copy-start(bf16[512,512]{1,0:T(8,128)(2,1)} %param.31) | copy-start | bytes 1572868
  298.6 2.3 copy-start.9
  298.6 2.3 copy-start.14
  299.8 56.2 %all-gather.6.cloned.1.call-start = ((), (), s32[]{:S(2)}) async-start(), calls=%async_computation.2 | async-start | bytes 2359296 | tf_op jit(solution)/shard_map/all_gather | solution.py:98
  300.9 84.8 %all-gather.8.cloned.1.call-start = ((), (), s32[]{:S(2)}) async-start(), calls=%async_computation.3 | async-start | bytes 2359296 | tf_op jit(solution)/shard_map/all_gather | solution.py:122
  302.0 118.7 %reduce-scatter.2.cloned.1.call-start = ((), (), s32[]{:S(2)}) async-start(), calls=%async_computation.4 | async-start | bytes 1310720 | tf_op jit(solution)/shard_map/reduce_scatter | solution.py:129
  385.8 7.4 %copy-start.16 = (u32[32]{0:T(128)S(1)}, u32[32]{0:T(128)}, u32[]{:S(2)}) copy-start(u32[32]{0:T(128)} %constant.53) | copy-start | bytes 388
  385.8 35.0 %copy-start.10 = (bf16[512,512]{1,0:T(8,128)(2,1)S(1)}, bf16[512,512]{1,0:T(8,128)(2,1)}, u32[]{:S(2)}) copy-start(bf16[512,512]{1,0:T(8,128)(2,1)} %param.34) | copy-start | bytes 1572868
  385.8 35.0 %copy-start.15 = (f32[512]{0:T(512)S(1)}, f32[512]{0:T(512)}, u32[]{:S(2)}) copy-start(f32[512]{0:T(512)} %param.35) | copy-start | bytes 6148
Sparse Core Ops, SparseCore 0:
  299.9 26.9 all-gather.3
  328.9 27.1 all-gather.5
  357.9 27.7 all-gather.7
  393.3 27.3 reduce-scatter.1
where the time goes:
time: 430 us; the launch traced here: 429 us
  blocking collectives  270 us (63%)
  waiting for transfers between devices  89.9 us (21%)
  matrix products  25.3 us (6%)
  between operations  14.3 us (3%)
  starting transfers between devices  13.9 us (3%)
  other arithmetic  11.1 us (3%)
  local copies, waits for them, and re-layouts  4.89 us (1%)
    psum x3, blocking collectives, group_norm(): sums = lax.psum(jnp.sum(grouped, axis=(0, 2)), ('tile', 'head'))  126 us
    psum x3, blocking collectives, group_norm(): lax.psum(jnp.sum(deviation * deviation, axis=(0, 2)), ('tile', 'head'))  121 us
    all_gather x1, waiting for transfers between devices, per_device(): key_rows = lax.all_gather(keys, 'tile', axis=0, tiled=True)  29.1 us
    all_gather x1, waiting for transfers between devices, per_device(): tile_queries = lax.all_gather(queries, 'head', axis=0, tiled=True)  24.9 us
    ppermute x4, waiting for transfers between devices, extended(): after = lax.ppermute(initial, axis, down)  15.9 us
    reduce_scatter x1, waiting for transfers between devices, per_device(): lax.psum_scatter((weighted * factor[:, None]).astype(jnp.bfloat16), 'head...  14.1 us
    unnamed x1, blocking collectives  12.1 us
    pmax x1, blocking collectives, per_device(): top = lax.pmax(run_max, 'head')  11.7 us
  transfers between devices with their start and end apart: 12, of which 8 were waited for; matrix products, arithmetic and copies ran while one was open for 4% of the time, Pallas kernels for 0%

commit v1 on v0

--- a/solution.py
+++ b/solution.py
@@ -82,7 +82,12 @@
     queries = (
         jnp.dot(normed, query_weight, preferred_element_type=jnp.float32) + query_bias
     ).astype(jnp.bfloat16)
-    tile_queries = lax.all_gather(queries, "head", axis=0, tiled=True)
+    ring = [queries]
+    for hop in range(3):
+        ring.append(lax.ppermute(ring[-1], "head", [(dev, (dev + 1) % 4) for dev in range(4)]))
+    tile_queries = jnp.roll(
+        jnp.concatenate(ring[::-1], axis=0), (lax.axis_index("head") + 1) * ring[0].shape[0], axis=0
+    )
     query_rows = tile_queries.shape[0]
     softmax_scale = 1.0 / C**0.5
     widest = positions * max(1, 2048 // positions)

time: 430 us -> 401 us (0.933)
  waiting for transfers between devices: 89.9 us -> 57.8 us
  local copies, waits for them, and re-layouts: 4.89 us -> 10.7 us
    all_gather x1, waiting for transfers between devices: 29.1 us -> 0.01 us  [per_device(): key_rows = lax.all_gather(keys, 'tile', axis=0, tiled=True)]
    all_gather x1 -> x0, waiting for transfers between devices: 24.9 us -> none  [per_device(): tile_queries = lax.all_gather(queries, 'head', axis=0, tiled=True)]
    ppermute x0 -> x3, waiting for transfers between devices: none -> 23.9 us  [per_device(): lax.ppermute(ring[-1], 'head', [(dev, (dev + 1) % 4) for dev in range(4)])]
    unnamed x39 -> x46, local copies, waits for them, and re-layouts: 1.84 us -> 6.89 us
  transfers between devices with their start and end apart: 12 -> 14, of which waited for: 8 -> 9; matrix products, arithmetic and copies ran while one was open for 4% -> 5% of each run, Pallas kernels for 0% -> 0%
where the time goes in v1:
time: 401 us; the launch traced here: 400 us
  blocking collectives  267 us (67%)
  waiting for transfers between devices  57.8 us (14%)
  matrix products  24.6 us (6%)
  starting transfers between devices  15.4 us (4%)
  between operations  14.3 us (4%)
  other arithmetic  10.8 us (3%)
  local copies, waits for them, and re-layouts  10.7 us (3%)
    psum x3, blocking collectives, group_norm(): sums = lax.psum(jnp.sum(grouped, axis=(0, 2)), ('tile', 'head'))  126 us
    psum x3, blocking collectives, group_norm(): lax.psum(jnp.sum(deviation * deviation, axis=(0, 2)), ('tile', 'head'))  121 us
    ppermute x3, waiting for transfers between devices, per_device(): lax.ppermute(ring[-1], 'head', [(dev, (dev + 1) % 4) for dev in range(4)])  23.9 us
    ppermute x4, waiting for transfers between devices, extended(): after = lax.ppermute(initial, axis, down)  15.9 us
    reduce_scatter x1, waiting for transfers between devices, per_device(): lax.psum_scatter((weighted * factor[:, None]).astype(jnp.bfloat16), 'head...  14.1 us
    unnamed x1, blocking collectives  12.1 us
    ppermute x4, starting transfers between devices, extended(): before = lax.ppermute(last, axis, up)  8.65 us
    pmax x1, blocking collectives, per_device(): top = lax.pmax(run_max, 'head')  8.35 us
  transfers between devices with their start and end apart: 14, of which 9 were waited for; matrix products, arithmetic and copies ran while one was open for 5% of the time, Pallas kernels for 0%

profile of v1, /device:TPU:0, one launch (start us, length us, event | category | flops | bytes accessed | tf_op | source)
XLA Modules:
  0.0 400.0 jit_solution(9726510197306035422)
XLA Ops:
  7.8 42.0 %psum.42 = f32[32]{0:T(128)S(1)} all-reduce(f32[32]{0:T(128)S(1)} %reduce_sum.83), channel_id=1, replica_groups=mesh['tile'=8,'head'=4] {'tile','head'}, use_global_device_ids=true, to_apply=%region_2.0 | all-reduce | flops 32 | bytes 256 | tf_op jit(solution)/shard_map/psum | solution.py:25
  51.2 40.1 %psum.43 = f32[32]{0:T(128)S(1)} all-reduce(f32[32]{0:T(128)S(1)} %reduce_sum.89), channel_id=1, replica_groups=mesh['tile'=8,'head'=4] {'tile','head'}, use_global_device_ids=true, to_apply=%region_5.6 | all-reduce | flops 32 | bytes 256 | tf_op jit(solution)/shard_map/psum | solution.py:28
  92.7 1.3 collective-permute-start
  94.0 1.3 collective-permute-start.1
  96.5 3.3 collective-permute-done.1
  99.8 2.6 collective-permute-start.2
  102.5 1.3 collective-permute-start.3
  103.8 4.2 %collective-permute-done.3 = bf16[4,1,512]{2,1,0:T(2,128)(2,1)S(1)} collective-permute-done((bf16[4,1,512]{2,1,0:T(2,128)(2,1)S(1)}, bf16[4,1,512]{2,1,0:T(2,128)(2,1)S(1)}, u32[]{:S(2)}, u32[]{:S(2)}) %collective-permute-start.3) | collective-permute-done | bytes 4128 | tf_op jit(solution)/shard_map/ppermute | solution.py:18
  108.8 1.5 select_reduce_fusion.1
  110.5 42.0 %psum.44 = f32[32]{0:T(128)S(1)} all-reduce(f32[32]{0:T(128)S(1)} %reduce_sum.92), channel_id=1, replica_groups=mesh['tile'=8,'head'=4] {'tile','head'}, use_global_device_ids=true, to_apply=%region_8.9 | all-reduce | flops 32 | bytes 256 | tf_op jit(solution)/shard_map/psum | solution.py:25
  153.5 39.9 %psum.45 = f32[32]{0:T(128)S(1)} all-reduce(f32[32]{0:T(128)S(1)} %reduce_sum.117), channel_id=1, replica_groups=mesh['tile'=8,'head'=4] {'tile','head'}, use_global_device_ids=true, to_apply=%region_11.12 | all-reduce | flops 32 | bytes 256 | tf_op jit(solution)/shard_map/psum | solution.py:28
  194.0 1.3 collective-permute-start.4
  195.3 1.3 collective-permute-start.5
  196.8 4.2 %collective-permute-done.5 = bf16[1,128,512]{2,1,0:T(8,128)(2,1)S(1)} collective-permute-done((bf16[1,128,512]{2,1,0:T(8,128)(2,1)S(1)}, bf16[1,128,512]{2,1,0:T(8,128)(2,1)S(1)}, u32[]{:S(2)}, u32[]{:S(2)}) %collective-permute-start.5) | collective-permute-done | bytes 131104 | tf_op jit(solution)/shard_map/ppermute | solution.py:18
  201.1 3.4 collective-permute-start.6
  204.5 1.3 collective-permute-start.7
  205.8 4.2 %collective-permute-done.7 = bf16[4,1,512]{2,1,0:T(2,128)(2,1)S(1)} collective-permute-done((bf16[4,1,512]{2,1,0:T(2,128)(2,1)S(1)}, bf16[4,1,512]{2,1,0:T(2,128)(2,1)S(1)}, u32[]{:S(2)}, u32[]{:S(2)}) %collective-permute-start.7) | collective-permute-done | bytes 4128 | tf_op jit(solution)/shard_map/ppermute | solution.py:18
  210.8 3.8 convolution_select_fusion
  215.9 41.5 %psum.46 = f32[32]{0:T(128)S(1)} all-reduce(f32[32]{0:T(128)S(1)} %reduce_sum.120), channel_id=1, replica_groups=mesh['tile'=8,'head'=4] {'tile','head'}, use_global_device_ids=true, to_apply=%region_14.15 | all-reduce | flops 32 | bytes 256 | tf_op jit(solution)/shard_map/psum | solution.py:25
  258.0 40.5 %psum.47 = f32[32]{0:T(128)S(1)} all-reduce(f32[32]{0:T(128)S(1)} %reduce_sum.123), channel_id=1, replica_groups=mesh['tile'=8,'head'=4] {'tile','head'}, use_global_device_ids=true, to_apply=%region_17.18 | all-reduce | flops 32 | bytes 256 | tf_op jit(solution)/shard_map/psum | solution.py:28
  301.4 1.5 collective-permute-start.8
  302.8 7.6 %collective-permute-done.8 = bf16[256,512]{1,0:T(8,128)(2,1)S(1)} collective-permute-done((bf16[256,512]{1,0:T(8,128)(2,1)S(1)}, bf16[256,512]{1,0:T(8,128)(2,1)S(1)}, u32[]{:S(2)}, u32[]{:S(2)}) %collective-permute-start.8) | collective-permute-done | bytes 262176 | tf_op jit(solution)/shard_map/ppermute | solution.py:87
  310.4 8.2 %collective-permute-done.9 = bf16[256,512]{1,0:T(8,128)(2,1)S(1)} collective-permute-done((bf16[256,512]{1,0:T(8,128)(2,1)S(1)}, bf16[256,512]{1,0:T(8,128)(2,1)S(1)}, u32[]{:S(2)}, u32[]{:S(2)}) %collective-permute-start.9) | collective-permute-done | bytes 262176 | tf_op jit(solution)/shard_map/ppermute | solution.py:87
  318.6 8.2 %collective-permute-done.10 = bf16[256,512]{1,0:T(8,128)(2,1)S(1)} collective-permute-done((bf16[256,512]{1,0:T(8,128)(2,1)S(1)}, bf16[256,512]{1,0:T(8,128)(2,1)S(1)}, u32[]{:S(2)}, u32[]{:S(2)}) %collective-permute-start.10) | collective-permute-done | bytes 262176 | tf_op jit(solution)/shard_map/ppermute | solution.py:87
  332.5 7.5 %multiply_reduce_fusion = (f32[1024]{0:T(1024)S(1)}, f32[1024,2048]{1,0:T(8,128)}) fusion(bf16[2048,512]{1,0:T(8,128)(2,1)} %all-gather.3.cloned.1.call-done, bf16[2048,512]{1,0:T(8,128)(2,1)} %constant_dynamic-update-slice_fusion, s32[]{:T(128)S(6)} %select_n.14), kind=kOutput, calls=%fused_computation.1 | convolution fusion | flops 2151676928 | bytes 11538436 | tf_op jit(solution)/shard_map/while/body/eval_jaxpr/dot_general | solution.py:114
  340.1 8.3 %pmax.7 = f32[1024]{0:T(1024)S(1)} all-reduce(f32[1024]{0:T(1024)S(1)} %broadcast_maximum_fusion), channel_id=1, replica_groups=mesh['tile'=8,'head'=4] {'head'}, use_global_device_ids=true, to_apply=%region_19.20 | all-reduce | flops 1024 | bytes 8192 | tf_op jit(solution)/shard_map/pmax | solution.py:131
  348.4 4.4 %fusion = f32[1024]{0:T(1024)S(1)} fusion(f32[1024,2048]{1,0:T(8,128)} %get-tuple-element.42, f32[1024]{0:T(1024)S(1)} %broadcast_maximum_fusion), kind=kLoop, calls=%fused_computation.2 | loop fusion | flops 6290432 | bytes 8396800 | tf_op jit(solution)/shard_map/while/body/eval_jaxpr/reduce_sum | solution.py:119
  352.8 3.7 all-gather.5.cloned.1.call-done
  356.5 7.4 %multiply_convert_fusion = bf16[1024,512]{1,0:T(8,128)(2,1)} fusion(bf16[2048,512]{1,0:T(8,128)(2,1)} %all-gather.5.cloned.1.call-done, f32[1024,2048]{1,0:T(8,128)} %get-tuple-element.42, f32[1024]{0:T(1024)S(1)} %broadcast_maximum_fusion, f32[1024]{0:T(1024)S(1)} %get-tuple-element.18, f32[1024]{0:T(1024)S(1)} %get-tuple-element.38), kind=kOutput, calls=%fused_computation.7 | convolution fusion | flops 2155347968 | bytes 11546624 | tf_op jit(solution)/shard_map/while/body/eval_jaxpr/dot_general | solution.py:120
  365.2 12.1 %all-reduce = bf16[1024]{0:T(1024)(128)(2,1)S(1)} all-reduce(bf16[1024]{0:T(1024)(128)(2,1)S(1)} %get-tuple-element.17), channel_id=3, replica_groups=mesh['tile'=8,'head'=4] {'head'}, use_global_device_ids=true, to_apply=%region_22.23.clone | all-reduce | flops 1024 | bytes 4096
  377.4 14.1 %reduce-scatter.2.cloned.1.call-done = bf16[256,512]{1,0:T(8,128)(2,1)} async-done(((bf16[1024,512]{1,0:T(8,128)(2,1)}), bf16[256,512]{1,0:T(8,128)(2,1)}) %reduce-scatter.2.cloned.1.call-update) | async-done | bytes 262160 | tf_op jit(solution)/shard_map/reduce_scatter | solution.py:134
  391.5 2.0 fusion.11
  (122 shorter events, 19.7 us)
Async XLA Ops:
  6.5 292.3 %copy-start = (bf16[512,512]{1,0:T(8,128)(2,1)S(1)}, bf16[512,512]{1,0:T(8,128)(2,1)}, u32[]{:S(2)}) copy-start(bf16[512,512]{1,0:T(8,128)(2,1)} %param.31) | copy-start | bytes 1572868
  6.5 326.0 %all-gather.3.cloned.1.call-start = ((), (), s32[]{:S(2)}) async-start(), calls=%async_computation.1 | async-start | bytes 2359296 | tf_op jit(solution)/shard_map/all_gather | solution.py:103
  92.7 3.8 collective-permute-start
  94.0 5.7 %collective-permute-start.1 = (bf16[1,128,512]{2,1,0:T(8,128)(2,1)S(1)}, bf16[1,128,512]{2,1,0:T(8,128)(2,1)S(1)}, u32[]{:S(2)}, u32[]{:S(2)}) collective-permute-start(bf16[1,128,512]{2,1,0:T(8,128)(2,1)S(1)} %get-tuple-element.37), channel_id=1, source_target_pairs={{4,0},{8,4},{12,8},{16,12},{20,16},{24,20},{28,24},{5,1},{9,5},{13... | collective-permute-start | bytes 393224 | tf_op jit(solution)/shard_map/ppermute | solution.py:18
  99.8 9.0 %copy-start.7 = (bf16[3,3,512,512]{3,2,1,0:T(8,128)(2,1)S(1)}, bf16[3,3,512,512]{3,2,1,0:T(8,128)(2,1)}, u32[]{:S(2)}) copy-start(bf16[3,3,512,512]{3,2,1,0:T(8,128)(2,1)} %param.21) | copy-start | bytes 14155780
  99.8 4.0 %collective-permute-start.2 = (bf16[4,1,512]{2,1,0:T(2,128)(2,1)S(1)}, bf16[4,1,512]{2,1,0:T(2,128)(2,1)S(1)}, u32[]{:S(2)}, u32[]{:S(2)}) collective-permute-start(bf16[4,1,512]{2,1,0:T(2,128)(2,1)S(1)} %get-tuple-element.32), channel_id=1, source_target_pairs={{0,1},{1,2},{2,3},{4,5},{5,6},{6,7},{8,9},{9,10},{10,11},{12,13},{... | collective-permute-start | bytes 12296 | tf_op jit(solution)/shard_map/ppermute | solution.py:17
  102.4 6.4 %copy-start.2 = (f32[512]{0:T(512)S(1)}, f32[512]{0:T(512)}, u32[]{:S(2)}) copy-start(f32[512]{0:T(512)} %param.22) | copy-start | bytes 6148
  102.4 6.4 %copy-start.6 = (pred[8,17]{0,1:T(8,128)(4,1)S(1)}, pred[8,17]{0,1:T(8,128)(4,1)}, u32[]{:S(2)}) copy-start(pred[8,17]{0,1:T(8,128)(4,1)} %constant.77) | copy-start | bytes 412
  102.5 5.5 %collective-permute-start.3 = (bf16[4,1,512]{2,1,0:T(2,128)(2,1)S(1)}, bf16[4,1,512]{2,1,0:T(2,128)(2,1)S(1)}, u32[]{:S(2)}, u32[]{:S(2)}) collective-permute-start(bf16[4,1,512]{2,1,0:T(2,128)(2,1)S(1)} %get-tuple-element.33), channel_id=1, source_target_pairs={{1,0},{2,1},{3,2},{5,4},{6,5},{7,6},{9,8},{10,9},{11,10},{13,12},{... | collective-permute-start | bytes 12296 | tf_op jit(solution)/shard_map/ppermute | solution.py:18
  110.3 83.4 %copy-start.3 = (f32[512]{0:T(512)S(1)}, f32[512]{0:T(512)}, u32[]{:S(2)}) copy-start(f32[512]{0:T(512)} %param.24) | copy-start | bytes 6148
  110.3 83.4 %copy-start.4 = (f32[512]{0:T(512)S(1)}, f32[512]{0:T(512)}, u32[]{:S(2)}) copy-start(f32[512]{0:T(512)} %param.23) | copy-start | bytes 6148
  194.0 2.8 collective-permute-start.4
  195.3 5.7 %collective-permute-start.5 = (bf16[1,128,512]{2,1,0:T(8,128)(2,1)S(1)}, bf16[1,128,512]{2,1,0:T(8,128)(2,1)S(1)}, u32[]{:S(2)}, u32[]{:S(2)}) collective-permute-start(bf16[1,128,512]{2,1,0:T(8,128)(2,1)S(1)} %get-tuple-element.35), channel_id=1, source_target_pairs={{4,0},{8,4},{12,8},{16,12},{20,16},{24,20},{28,24},{5,1},{9,5},{13... | collective-permute-start | bytes 393224 | tf_op jit(solution)/shard_map/ppermute | solution.py:18
  201.1 4.8 %collective-permute-start.6 = (bf16[4,1,512]{2,1,0:T(2,128)(2,1)S(1)}, bf16[4,1,512]{2,1,0:T(2,128)(2,1)S(1)}, u32[]{:S(2)}, u32[]{:S(2)}) collective-permute-start(bf16[4,1,512]{2,1,0:T(2,128)(2,1)S(1)} %get-tuple-element.28), channel_id=1, source_target_pairs={{0,1},{1,2},{2,3},{4,5},{5,6},{6,7},{8,9},{9,10},{10,11},{12,13},{... | collective-permute-start | bytes 12296 | tf_op jit(solution)/shard_map/ppermute | solution.py:17
  204.5 5.5 %collective-permute-start.7 = (bf16[4,1,512]{2,1,0:T(2,128)(2,1)S(1)}, bf16[4,1,512]{2,1,0:T(2,128)(2,1)S(1)}, u32[]{:S(2)}, u32[]{:S(2)}) collective-permute-start(bf16[4,1,512]{2,1,0:T(2,128)(2,1)S(1)} %get-tuple-element.30), channel_id=1, source_target_pairs={{1,0},{2,1},{3,2},{5,4},{6,5},{7,6},{9,8},{10,9},{11,10},{13,12},{... | collective-permute-start | bytes 12296 | tf_op jit(solution)/shard_map/ppermute | solution.py:18
  214.6 1.0 copy-start.1
  214.6 0.9 copy-start.5
  215.1 83.7 %copy-start.12 = (f32[512]{0:T(512)S(1)}, f32[512]{0:T(512)}, u32[]{:S(2)}) copy-start(f32[512]{0:T(512)} %param.28) | copy-start | bytes 6148
  215.1 83.7 %copy-start.13 = (f32[512]{0:T(512)S(1)}, f32[512]{0:T(512)}, u32[]{:S(2)}) copy-start(f32[512]{0:T(512)} %param.27) | copy-start | bytes 6148
  215.7 84.2 %copy-start.8 = (bf16[512,512]{1,0:T(8,128)(2,1)S(1)}, bf16[512,512]{1,0:T(8,128)(2,1)}, u32[]{:S(2)}) copy-start(bf16[512,512]{1,0:T(8,128)(2,1)} %param.32) | copy-start | bytes 1572868
  215.7 84.2 %copy-start.11 = (f32[512]{0:T(512)S(1)}, f32[512]{0:T(512)}, u32[]{:S(2)}) copy-start(f32[512]{0:T(512)} %param.33) | copy-start | bytes 6148
  298.7 2.3 copy-start.9
  298.7 2.3 copy-start.14
  299.9 56.7 %all-gather.5.cloned.1.call-start = ((), (), s32[]{:S(2)}) async-start(), calls=%async_computation.2 | async-start | bytes 2359296 | tf_op jit(solution)/shard_map/all_gather | solution.py:127
  301.0 90.5 %reduce-scatter.2.cloned.1.call-start = ((), (), s32[]{:S(2)}) async-start(), calls=%async_computation.3 | async-start | bytes 1310720 | tf_op jit(solution)/shard_map/reduce_scatter | solution.py:134
  301.4 9.1 %collective-permute-start.8 = (bf16[256,512]{1,0:T(8,128)(2,1)S(1)}, bf16[256,512]{1,0:T(8,128)(2,1)S(1)}, u32[]{:S(2)}, u32[]{:S(2)}) collective-permute-start(bf16[256,512]{1,0:T(8,128)(2,1)S(1)} %fusion.12), channel_id=1, source_target_pairs={{0,1},{1,2},{2,3},{3,0},{4,5},{5,6},{6,7},{7,4},{8,9},{9,10},{10,1... | collective-permute-start | bytes 786440 | tf_op jit(solution)/shard_map/ppermute | solution.py:87
  310.4 8.2 %collective-permute-start.9 = (bf16[256,512]{1,0:T(8,128)(2,1)S(1)}, bf16[256,512]{1,0:T(8,128)(2,1)S(1)}, u32[]{:S(2)}, u32[]{:S(2)}) collective-permute-start(bf16[256,512]{1,0:T(8,128)(2,1)S(1)} %collective-permute-done.8), channel_id=1, source_target_pairs={{0,1},{1,2},{2,3},{3,0},{4,5},{5,6},{6,7},{7,4},{8,9},{9,10},{10,1... | collective-permute-start | bytes 786440 | tf_op jit(solution)/shard_map/ppermute | solution.py:87
  318.6 8.2 %collective-permute-start.10 = (bf16[256,512]{1,0:T(8,128)(2,1)S(1)}, bf16[256,512]{1,0:T(8,128)(2,1)S(1)}, u32[]{:S(2)}, u32[]{:S(2)}) collective-permute-start(bf16[256,512]{1,0:T(8,128)(2,1)S(1)} %collective-permute-done.9), channel_id=1, source_target_pairs={{0,1},{1,2},{2,3},{3,0},{4,5},{5,6},{6,7},{7,4},{8,9},{9,10},{10,1... | collective-permute-start | bytes 786440 | tf_op jit(solution)/shard_map/ppermute | solution.py:87
  356.5 7.4 %copy-start.16 = (u32[32]{0:T(128)S(1)}, u32[32]{0:T(128)}, u32[]{:S(2)}) copy-start(u32[32]{0:T(128)} %constant.83) | copy-start | bytes 388
  356.5 35.0 %copy-start.10 = (bf16[512,512]{1,0:T(8,128)(2,1)S(1)}, bf16[512,512]{1,0:T(8,128)(2,1)}, u32[]{:S(2)}) copy-start(bf16[512,512]{1,0:T(8,128)(2,1)} %param.34) | copy-start | bytes 1572868
  356.5 35.0 %copy-start.15 = (f32[512]{0:T(512)S(1)}, f32[512]{0:T(512)}, u32[]{:S(2)}) copy-start(f32[512]{0:T(512)} %param.35) | copy-start | bytes 6148
Sparse Core Ops, SparseCore 0:
  300.0 26.7 all-gather.2
  328.7 27.7 all-gather.4
  364.1 27.3 reduce-scatter.1
